TPU v7x, 128 devices: a whole 4x4x4 slice. The times are simulated.
128 devices in a mesh: blk: 32 (over z, y, core), rep: 4 (over x).
Axes of the slice: x: 4, y: 4, z: 4, core: 2. Of those that a mesh axis runs over, the one named last changes fastest.
Arguments:
- source_blocks: bfloat16 [256, 1024, 1024], P('blk', 'rep'), may hold values from -6 to 6
- coefficients: float32 [256, 2], P('blk'), may hold values from 0.3 to 1
- target_sector: int32 [256, 2], P('blk'), may hold values from 0 to 127, as said below
Outputs:
- recoupled: bfloat16 [128, 1024, 1024], P('blk', 'rep')
- density: float32 [128, 1024, 1024], P('blk', None, 'rep')
Inputs may be any that keep to these rules, and one draw needn't show every extreme that they name: `target_sector`: sector t is owned by index t // 4 of blk. The 16 entries of one index of blk name sectors of any one owner at most 1 times, counted with repeats; one owner, the same for all indices, is named exactly 1 times by each index. A row never names one sector twice.
All inputs are finite; a program needn't handle non-finite values.
Results may differ from a plain program's by a relative error of at most 0.009.
Values may be sent and summed in bfloat16 or wider, within the bound.
A program may use at most 320 MiB of HBM per device.

v0:
```python
import jax
import jax.numpy as jnp
from jax import lax
from jax.sharding import PartitionSpec as P

TGT_DEV = 4


def body(source_blocks, coefficients, target_sector):
    groups = lax.axis_size("blk")
    sources, height, breadth = source_blocks.shape
    columns_each = coefficients.shape[1]
    entries = sources * columns_each
    capacity = max(1, 2 * entries // groups)
    slot_total = groups * capacity
    flat_target = target_sector.reshape(entries)
    owners = flat_target // TGT_DEV
    within = flat_target % TGT_DEV
    positions = jnp.arange(entries, dtype=jnp.int32)
    earlier = (owners[None, :] == owners[:, None]) & (positions[None, :] < positions[:, None])
    ordinal = jnp.sum(earlier.astype(jnp.int32), axis=1)
    slot_of = owners * capacity + ordinal
    placing = slot_of[None, :] == jnp.arange(slot_total, dtype=jnp.int32)[:, None]
    filled = jnp.any(placing, axis=1)
    picked = jnp.sum(placing.astype(jnp.int32) * positions[None, :], axis=1)
    contribution = (
        coefficients[:, :, None, None] * source_blocks[:, None].astype(jnp.float32)
    ).astype(jnp.bfloat16)
    contribution = contribution.reshape(entries, height, breadth)
    outgoing = jnp.where(filled[:, None, None], contribution[picked], jnp.zeros((), jnp.bfloat16))
    sector_onehot = (within[:, None] == jnp.arange(TGT_DEV, dtype=jnp.int32)[None, :]).astype(
        jnp.float32
    )
    labels = jnp.dot(placing.astype(jnp.float32), sector_onehot).astype(jnp.bfloat16)
    incoming, in_labels = (
        lax.all_to_all(outgoing, "blk", split_axis=0, concat_axis=0, tiled=True),
        lax.all_to_all(labels, "blk", split_axis=0, concat_axis=0, tiled=True),
    )
    recoupled = jnp.einsum(
        "xt,xrd->trd", in_labels, incoming, preferred_element_type=jnp.float32
    ).astype(jnp.bfloat16)
    partial_gram = jnp.einsum(
        "trc,trd->tcd", recoupled, recoupled, preferred_element_type=jnp.float32
    )
    density = lax.psum_scatter(
        partial_gram.astype(jnp.bfloat16), "rep", scatter_dimension=2, tiled=True
    ).astype(jnp.float32)
    return (recoupled, density)


def solution(mesh):
    in_specs = (P("blk", "rep", None), P("blk", None), P("blk", None))
    out_specs = (P("blk", "rep", None), P("blk", None, "rep"))
    return jax.shard_map(body, mesh=mesh, in_specs=in_specs, out_specs=out_specs, check_vma=False)
```

profile of v0, /device:TPU:0, one launch (start us, length us, event | category | flops | bytes accessed | tf_op | source)
XLA Modules:
  0.0 397.7 jit_solution(8010733594596586574)
XLA Ops:
  7.2 0.8 copy.24
  7.9 0.1 reshape.119
  8.0 0.2 convert_reduce_fusion
  8.2 0.3 fusion.6
  8.5 0.7 copy.25
  9.2 8.4 %all-to-all-start = ((bf16[32,1,4]{2,1,0:T(2,128)(2,1)}), bf16[32,1,4]{2,1,0:T(2,128)(2,1)S(1)}, u32[]{:S(2)}, u32[]{:S(2)}) async-start(bf16[32,1,4]{2,1,0:T(2,128)(2,1)} %copy.25), calls=%async_computation | async-start | bytes 32768 | tf_op jit(solution)/shard_map/all_to_all | solution.py:37
  17.6 0.1 select_reduce_fusion
  17.7 0.1 fusion.7
  17.8 0.8 copy.27
  18.6 0.1 mul.26
  18.7 6.5 %convert_element_type.28 = f32[8,256,1024]{2,1,0:T(8,128)} convert(bf16[8,256,1024]{2,1,0:T(8,128)(2,1)} %param.3) | non-fusion elementwise | flops 2097152 | bytes 12582912 | tf_op jit(solution)/shard_map/convert_element_type | solution.py:27
  25.1 8.7 %fusion = bf16[16,256,1024]{2,1,0:T(8,128)(2,1)} fusion(f32[8,256,1024]{2,1,0:T(8,128)} %convert_element_type.28, f32[16]{0:T(128)S(1)} %mul.26), kind=kLoop, calls=%fused_computation.2 | loop fusion | flops 8388608 | bytes 16777280 | tf_op jit(solution)/shard_map/convert_element_type | solution.py:28
  33.8 10.6 %gather_fusion = bf16[32,256,1024]{2,1,0:T(8,128)(2,1)} fusion(bf16[16,256,1024]{2,1,0:T(8,128)(2,1)} %fusion, s32[1024]{0:T(1024)S(1)} %pad_clamp_fusion), kind=kCustom, calls=%fused_computation | custom fusion | bytes 33554560 | tf_op jit(solution)/shard_map/gather | solution.py:30
  44.4 14.0 %broadcast_select_fusion = bf16[32,256,1024]{2,1,0:T(8,128)(2,1)} fusion(bf16[32,256,1024]{2,1,0:T(8,128)(2,1)} %gather_fusion, pred[32]{0:T(512)(128)(4,1)S(1)} %fusion.7), kind=kLoop, calls=%fused_computation.5 | loop fusion | flops 8388608 | bytes 33554464 | tf_op jit(solution)/shard_map/jit(_where)/select_n | solution.py:30
  58.3 7.5 %all-to-all-start.1 = ((bf16[32,256,1024]{2,1,0:T(8,128)(2,1)}), bf16[32,256,1024]{2,1,0:T(8,128)(2,1)}, u32[]{:S(2)}, u32[]{:S(2)}) async-start(bf16[32,256,1024]{2,1,0:T(8,128)(2,1)} %broadcast_select_fusion), calls=%async_computation.1 | async-start | bytes 33554432 | tf_op jit(solution)/shard_map/all_to_all | solution.py:36
  65.8 0.2 reduce-scatter.2.cloned.1.call-start
  66.1 0.1 copy.26
  66.2 212.9 %all-to-all-done.1 = bf16[32,256,1024]{2,1,0:T(8,128)(2,1)} async-done(((bf16[32,256,1024]{2,1,0:T(8,128)(2,1)}), bf16[32,256,1024]{2,1,0:T(8,128)(2,1)}, u32[]{:S(2)}, u32[]{:S(2)}) %all-to-all-start.1) | async-done | bytes 16777248 | tf_op jit(solution)/shard_map/all_to_all | solution.py:36
  279.1 24.1 %fusion.3 = bf16[4,256,1024]{2,0,1:T(4,128)(2,1)S(1)} fusion(bf16[32,256,1024]{2,1,0:T(8,128)(2,1)} %all-to-all-done.1, bf16[32,1,4]{0,2,1:T(4,128)(2,1)S(1)} %copy.26), kind=kOutput, calls=%fused_computation.7 | convolution fusion | flops 68157440 | bytes 18874624 | tf_op jit(solution)/shard_map/xt,xrd->trd/dot_general | solution.py:39
  303.2 0.6 copy.31
  303.9 5.6 %convolution_convert_fusion = bf16[4,1024,1024]{2,1,0:T(8,128)(2,1)} fusion(bf16[4,256,1024]{2,1,0:T(8,128)(2,1)S(1)} %copy.31), kind=kOutput, calls=%fused_computation.6 | convolution fusion | flops 2151677952 | bytes 10485760 | tf_op jit(solution)/shard_map/trc,trd->tcd/dot_general | solution.py:42
  309.5 0.0 reduce-scatter.2.cloned.1.call-update
  309.5 77.4 %reduce-scatter.2.cloned.1.call-done = bf16[4,1024,256]{2,1,0:T(8,128)(2,1)} async-done(((bf16[4,1024,1024]{2,1,0:T(8,128)(2,1)}), bf16[4,1024,256]{2,1,0:T(8,128)(2,1)}) %reduce-scatter.2.cloned.1.call-update) | async-done | bytes 2097168 | tf_op jit(solution)/shard_map/reduce_scatter | solution.py:45
  386.9 4.0 convert_element_type.32
  (7 shorter events, 0.0 us)
Async XLA Ops:
  9.2 49.2 %all-to-all-start = ((bf16[32,1,4]{2,1,0:T(2,128)(2,1)}), bf16[32,1,4]{2,1,0:T(2,128)(2,1)S(1)}, u32[]{:S(2)}, u32[]{:S(2)}) async-start(bf16[32,1,4]{2,1,0:T(2,128)(2,1)} %copy.25), calls=%async_computation | async-start | bytes 32768 | tf_op jit(solution)/shard_map/all_to_all | solution.py:37
  58.3 220.7 %all-to-all-start.1 = ((bf16[32,256,1024]{2,1,0:T(8,128)(2,1)}), bf16[32,256,1024]{2,1,0:T(8,128)(2,1)}, u32[]{:S(2)}, u32[]{:S(2)}) async-start(bf16[32,256,1024]{2,1,0:T(8,128)(2,1)} %broadcast_select_fusion), calls=%async_computation.1 | async-start | bytes 33554432 | tf_op jit(solution)/shard_map/all_to_all | solution.py:36
  65.8 321.1 %reduce-scatter.2.cloned.1.call-start = ((), (), s32[]{:S(2)}) async-start(), calls=%async_computation.3 | async-start | bytes 10485760 | tf_op jit(solution)/shard_map/reduce_scatter | solution.py:45
  303.8 5.6 %copy-start = (bf16[4,256,1024]{2,1,0:T(8,128)(2,1)}, bf16[4,256,1024]{2,1,0:T(8,128)(2,1)S(1)}, u32[]{:S(2)}) copy-start(bf16[4,256,1024]{2,1,0:T(8,128)(2,1)S(1)} %copy.31) | copy-start | bytes 6291460
Sparse Core Ops, SparseCore 0:
  309.6 77.2 reduce-scatter.1
where the time goes:
time: 399 us; the launch traced here: 398 us
  waiting for transfers between devices  290 us (73%)
  other arithmetic  33.5 us (8%)
  matrix products  30 us (8%)
  starting transfers between devices  16.1 us (4%)
  between operations  14.1 us (4%)
  local copies, waits for them, and re-layouts  13.7 us (3%)
    all_to_all x1, waiting for transfers between devices, body(): lax.all_to_all(outgoing, 'blk', split_axis=0, concat_axis=0, tiled=True)  213 us
    reduce_scatter x1, waiting for transfers between devices, body(): lax.psum_scatter(partial_gram.astype(jnp.bfloat16), 'rep', scatter_dimens...  77.4 us
    dot_general x1, matrix products, body(): jnp.einsum('xt,xrd->trd', in_labels, incoming, preferred_element_type=jnp...  24.1 us
    select_n x1, other arithmetic, body(): jnp.where(filled[:, None, None], contribution[picked], jnp.zeros((), jnp....  14 us
    gather x1, local copies, waits for them, and re-layouts, body(): contribution[picked]  10.6 us
    convert_element_type x1, other arithmetic, body(): contribution = (coefficients[:, :, None, None] * source_blocks[:, None].a...  8.68 us
    all_to_all x1, starting transfers between devices, body(): lax.all_to_all(labels, 'blk', split_axis=0, concat_axis=0, tiled=True)  8.45 us
  transfers between devices with their start and end apart: 3, of which 2 were waited for; matrix products, arithmetic and copies ran while one was open for 10% of the time, Pallas kernels for 0%

commit v1 on v0

v1 whole, which is shorter than its diff:
```python
import functools

import jax
import jax.numpy as jnp
from jax import lax
from jax.experimental import pallas as pl
from jax.experimental.pallas import tpu as pltpu
from jax.sharding import PartitionSpec as P

MESH = pl.DeviceIdType.MESH
BF = jnp.bfloat16
F32 = jnp.float32

ROWS = 16
CW = 256
HALF = 128
HCOL = 512
NCC = HCOL // CW
NCH = (HALF // ROWS) * NCC
L_A2, L_CB, L_R2, L_FN, L_X2 = 2, 4, 6, 8, 10
STEPS = NCH + L_X2
OFFS = (0, 1, 3, 2)


def kernel(src, tbl, rec_out, den_out, G, TB, W, PS, T, F, Q, RG, D,
           s_in, s_a1, s_a2, s_r1, s_r2, s_d, s_x1, s_x2, s_t,
           n_in, n_a1, n_a2, n_r1, n_r2, n_d, n_x1, n_x2, n_t, s_out):
    blk = lax.axis_index("blk")
    x = lax.axis_index("rep")
    z = blk // 8
    y = (blk // 2) % 4
    c = blk % 2
    oc = 1 - c

    def at_z(k, core):
        return ((((z + k) % 4) * 4 + y) * 2 + core, x)

    def at_y(k, core):
        return ((z * 4 + (y + k) % 4) * 2 + core, x)

    def at_x(k, core):
        return ((z * 4 + y) * 2 + core, (x + k) % 4)

    partner = (blk + 1 - 2 * c, x)
    gather_at = (at_z, at_y)
    scatter_at = (at_y, at_z)

    def rcopy(a, b, ssem, rsem, dev):
        pltpu.make_async_remote_copy(
            src_ref=a, dst_ref=b, send_sem=ssem, recv_sem=rsem,
            device_id=dev, device_id_type=MESH).start()

    def waiter(ref, ssem, rsem):
        return pltpu.make_async_remote_copy(
            src_ref=ref, dst_ref=ref, send_sem=ssem, recv_sem=rsem,
            device_id=partner, device_id_type=MESH)

    def got(ref, sem):
        waiter(ref, n_d.at[0], sem).wait_recv()

    def sent(ref, sem):
        waiter(ref, sem, s_d.at[0]).wait_send()

    peers = [partner]
    for k in (1, 2, 3):
        for core in (0, 1):
            peers.append(at_z(k, core))
            peers.append(at_y(k, core))
    for k in (1, 3):
        for core in (0, 1):
            peers.append(at_x(k, core))
    barrier = pltpu.get_barrier_semaphore()
    for dev in peers:
        pl.semaphore_signal(barrier, inc=1, device_id=dev, device_id_type=MESH)
    pl.semaphore_wait(barrier, len(peers))

    def place(q):
        rc = q // NCC
        cc = q % NCC
        r0 = pl.multiple_of(rc * ROWS, ROWS)
        c0 = pl.multiple_of(cc * CW, CW)
        return r0, c0, pl.ds(r0, ROWS), pl.ds(c0, CW)

    for p in range(2):
        rcopy(tbl, TB.at[p, 0, c], n_t.at[0], s_t.at[0], partner)
        for slot in (1, 2, 3):
            for core in (0, 1):
                rcopy(tbl, TB.at[p, slot, c], n_t.at[1], s_t.at[1],
                      gather_at[p](OFFS[slot], core))

    def load(q, carry):
        r0, c0, rows, cols = place(q)
        for p in range(2):
            cs = pl.ds(pl.multiple_of(p * HCOL + c0, CW), CW)
            mine = src.at[:, pl.ds(pl.multiple_of(c * HALF + r0, ROWS), ROWS), cs]
            other = src.at[:, pl.ds(pl.multiple_of(oc * HALF + r0, ROWS), ROWS), cs]
            dst = G.at[p, 0, pl.ds(c * 8, 8), rows, cols]
            pltpu.make_async_copy(mine, dst, s_in.at[q]).start()
            rcopy(other, dst, n_in.at[0], s_in.at[q], partner)
        return carry

    lax.fori_loop(0, NCH, load, 0)

    def stage_a1(q):
        _, _, rows, cols = place(q)
        got(G.at[:, 0, :, rows, cols], s_in.at[q])
        for p in range(2):
            mine = G.at[p, 0, :, rows, cols]
            rcopy(mine, G.at[p, 1, :, rows, cols], n_a1.at[0], s_a1.at[q], gather_at[p](1, c))
            rcopy(mine, G.at[p, 2, :, rows, cols], n_a1.at[1], s_a1.at[q], gather_at[p](3, c))

    def stage_a2(q):
        _, _, rows, cols = place(q)
        got(G.at[:, 1:3, :, rows, cols], s_a1.at[q])
        for p in range(2):
            rcopy(G.at[p, 1, 0:8, rows, cols], G.at[p, 3, 0:8, rows, cols],
                  n_a2.at[0], s_a2.at[q], gather_at[p](1, c))
            rcopy(G.at[p, 2, 8:16, rows, cols], G.at[p, 3, 8:16, rows, cols],
                  n_a2.at[1], s_a2.at[q], gather_at[p](3, c))

    def stage_cb(q):
        _, _, rows, cols = place(q)
        got(G.at[:, 3, :, rows, cols], s_a2.at[q])
        for p in range(2):
            s = G[p, :, :, rows, cols].reshape(64 * ROWS, CW)
            o = jnp.dot(W[p], s, preferred_element_type=F32)
            PS[p, :, :, rows, cols] = o.reshape(4, 8, ROWS, CW).astype(BF)
        for p in range(2):
            rcopy(PS.at[p, 3, 0:4, rows, cols], T.at[p, 0, :, rows, cols],
                  n_r1.at[0], s_r1.at[q], scatter_at[p](1, c))
            rcopy(PS.at[p, 3, 4:8, rows, cols], T.at[p, 1, :, rows, cols],
                  n_r1.at[1], s_r1.at[q], scatter_at[p](3, c))

    def stage_r2(q):
        _, _, rows, cols = place(q)
        got(T.at[:, :, :, rows, cols], s_r1.at[q])
        for p in range(2):
            a = PS[p, 1, 0:4, rows, cols].astype(F32) + T[p, 0, :, rows, cols].astype(F32)
            PS[p, 1, 0:4, rows, cols] = a.astype(BF)
            b = PS[p, 2, 4:8, rows, cols].astype(F32) + T[p, 1, :, rows, cols].astype(F32)
            PS[p, 2, 4:8, rows, cols] = b.astype(BF)
        for p in range(2):
            rcopy(PS.at[p, 1, :, rows, cols], F.at[p, 0, :, rows, cols],
                  n_r2.at[0], s_r2.at[q], scatter_at[p](1, c))
            rcopy(PS.at[p, 2, :, rows, cols], F.at[p, 1, :, rows, cols],
                  n_r2.at[1], s_r2.at[q], scatter_at[p](3, c))

    def stage_fn(q):
        _, _, rows, cols = place(q)
        got(F.at[:, :, :, rows, cols], s_r2.at[q])
        for p in range(2):
            for which in (oc, c):
                ks = pl.ds(which * 4, 4)
                v = (PS[p, 0, ks, rows, cols].astype(F32)
                     + F[p, 0, ks, rows, cols].astype(F32)
                     + F[p, 1, ks, rows, cols].astype(F32)).astype(BF)
                if which is c:
                    RG[0, :, c, p, rows, cols] = v
                else:
                    Q[:, p, rows, cols] = v
        away = Q.at[:, :, rows, cols]
        kept = RG.at[0, :, c, :, rows, cols]
        for slot, k in ((1, 1), (2, 3)):
            dst = RG.at[slot, :, c, :, rows, cols]
            rcopy(away, dst, n_x1.at[slot - 1], s_x1.at[q], at_x(k, oc))
            rcopy(kept, dst, n_x1.at[slot - 1], s_x1.at[q], at_x(k, c))
        rcopy(away, kept, n_d.at[0], s_d.at[q], partner)

    def stage_x2(q):
        _, _, rows, cols = place(q)
        got(RG.at[1:3, :, :, :, rows, cols], s_x1.at[q])
        rcopy(RG.at[1, :, 0, :, rows, cols], RG.at[3, :, 0, :, rows, cols],
              n_x2.at[0], s_x2.at[q], at_x(1, c))
        rcopy(RG.at[2, :, 1, :, rows, cols], RG.at[3, :, 1, :, rows, cols],
              n_x2.at[1], s_x2.at[q], at_x(3, c))

    def run(stage, q):
        @pl.when((q >= 0) & (q < NCH))
        def _():
            stage(q)

    stage_a1(0)
    stage_a1(1)

    got(TB.at[:, 0, 0], s_t.at[0])
    got(TB.at[:, 1:4], s_t.at[1])
    for p in range(2):
        TB[p, 0, c] = tbl[...]
    row = lax.broadcasted_iota(jnp.int32, (128, 128), 0)
    lane = lax.broadcasted_iota(jnp.int32, (128, 128), 1)
    same = (row % ROWS) == (lane % ROWS)
    sect = row // ROWS
    for p in range(2):
        for d in range(4):
            if p == 0:
                base = (z * 4 + (y + OFFS[d]) % 4) * 8
            else:
                base = (((z + OFFS[d]) % 4) * 4 + y) * 8
            want = (sect + base).astype(F32)

            def build(jk, carry, p=p, d=d, want=want):
                tab = TB[p, jk // 2, jk % 2]
                w = jnp.where(same & (tab[0:1, :] == want), tab[2:3, :], 0.0)
                w = w + jnp.where(same & (tab[1:2, :] == want), tab[3:4, :], 0.0)
                W[p, d * 128:(d + 1) * 128, pl.ds(pl.multiple_of(jk * 128, 128), 128)] = w.astype(BF)
                return carry

            lax.fori_loop(0, 8, build, 0)

    def step(s, carry):
        run(stage_a1, s + 2)
        run(stage_a2, s + 2 - L_A2)
        run(stage_x2, s + 2 - L_X2)
        run(stage_fn, s + 2 - L_FN)
        run(stage_r2, s + 2 - L_R2)
        run(stage_cb, s + 2 - L_CB)
        return carry

    lax.fori_loop(0, STEPS - 2, step, 0)

    def last_d(q, carry):
        _, _, rows, cols = place(q)
        got(RG.at[0, :, oc, :, rows, cols], s_d.at[q])
        return carry

    lax.fori_loop(0, NCH, last_d, 0)
    outs = []
    for h in range(2):
        for p in range(2):
            cp = pltpu.make_async_copy(
                RG.at[0, :, h, p],
                rec_out.at[:, h * HALF:(h + 1) * HALF, p * HCOL:(p + 1) * HCOL],
                s_out.at[h * 2 + p])
            cp.start()
            outs.append(cp)

    def last_x(q, carry):
        _, _, rows, cols = place(q)
        got(RG.at[3, :, :, :, rows, cols], s_x2.at[q])
        return carry

    lax.fori_loop(0, NCH, last_x, 0)

    xp = x // 2
    xo = pl.multiple_of((x % 2) * 256, 256)

    def gram(w, carry):
        rhs = RG[:, w, :, xp, :, pl.ds(xo, 256)].reshape(1024, 256)
        for p in range(2):
            lhs = RG[:, w, :, p].reshape(1024, HCOL)
            D[w, p * HCOL:(p + 1) * HCOL, :] = lax.dot_general(
                lhs, rhs, (((0,), (0,)), ((), ())), preferred_element_type=F32)
        pltpu.make_async_copy(D.at[w], den_out.at[w], s_out.at[4 + w]).start()
        return carry

    lax.fori_loop(0, 4, gram, 0)

    for w in range(4):
        pltpu.make_async_copy(D.at[w], den_out.at[w], s_out.at[4 + w]).wait()
    for cp in outs:
        cp.wait()

    sent(TB.at[:, 0, 0], n_t.at[0])
    sent(TB.at[:, 1:4], n_t.at[1])
    sent(src.at[:, 0:HALF, :], n_in.at[0])
    for k in range(2):
        sent(G.at[:, 0], n_a1.at[k])
        sent(G.at[:, 3, 0:8], n_a2.at[k])
        sent(T.at[:, 0], n_r1.at[k])
        sent(F.at[:, 0], n_r2.at[k])
        sent(RG.at[1], n_x1.at[k])
        sent(Q, n_x2.at[k])
    sent(Q, n_d.at[0])


def body(source_blocks, coefficients, target_sector):
    tab = jnp.concatenate([target_sector.T.astype(F32), coefficients.T], axis=0)
    tab = jnp.pad(jnp.repeat(tab, ROWS, axis=1), ((0, 4), (0, 0)))
    dma = pltpu.SemaphoreType.DMA
    chunk_sems = [dma((NCH,)) for _ in range(8)]
    return pl.pallas_call(
        kernel,
        out_shape=(jax.ShapeDtypeStruct((4, 256, 1024), BF),
                   jax.ShapeDtypeStruct((4, 1024, 256), F32)),
        in_specs=[pl.BlockSpec(memory_space=pl.ANY),
                  pl.BlockSpec(memory_space=pltpu.VMEM)],
        out_specs=(pl.BlockSpec(memory_space=pl.ANY),
                   pl.BlockSpec(memory_space=pl.ANY)),
        scratch_shapes=[
            pltpu.VMEM((2, 4, 16, HALF, HCOL), BF),
            pltpu.VMEM((2, 4, 2, 8, 128), F32),
            pltpu.VMEM((2, 512, 1024), BF),
            pltpu.VMEM((2, 4, 8, HALF, HCOL), BF),
            pltpu.VMEM((2, 2, 4, HALF, HCOL), BF),
            pltpu.VMEM((2, 2, 8, HALF, HCOL), BF),
            pltpu.VMEM((4, 2, HALF, HCOL), BF),
            pltpu.VMEM((4, 4, 2, 2, HALF, HCOL), BF),
            pltpu.VMEM((4, 1024, 256), F32),
            *chunk_sems,
            dma((2,)),
            dma((1,)), dma((2,)), dma((2,)), dma((2,)), dma((2,)), dma((1,)),
            dma((2,)), dma((2,)), dma((2,)),
            dma((8,)),
        ],
        compiler_params=pltpu.CompilerParams(
            collective_id=0, has_side_effects=True, vmem_limit_bytes=64 * 1024 * 1024 - 65536),
        name="recouple",
    )(source_blocks, tab)


def solution(mesh):
    in_specs = (P("blk", "rep", None), P("blk", None), P("blk", None))
    out_specs = (P("blk", "rep", None), P("blk", None, "rep"))
    return jax.shard_map(body, mesh=mesh, in_specs=in_specs, out_specs=out_specs, check_vma=False)
```

time: 399 us -> 146 us (0.37)
  waiting for transfers between devices: 290 us -> 0 us
  Pallas kernels: 0 us -> 138 us
  other arithmetic: 33.5 us -> 1.37 us
  matrix products: 30 us -> 0 us
  starting transfers between devices: 16.1 us -> 0 us
  between operations: 14.1 us -> 0.65 us
  local copies, waits for them, and re-layouts: 13.7 us -> 6.01 us
    all_to_all x2 -> x0, waiting for transfers between devices: 213 us -> none  [the longest x1 213 us: body(): lax.all_to_all(outgoing, 'blk', split_axis=0, concat_axis=0, tiled=True)]
    pallas_call x0 -> x1, Pallas kernels: none -> 138 us  [body(): pl.pallas_call(kernel, out_shape=(jax.ShapeDtypeStruct((4, 256, 1024), BF...]
    reduce_scatter x1 -> x0, waiting for transfers between devices: 77.4 us -> none  [body(): lax.psum_scatter(partial_gram.astype(jnp.bfloat16), 'rep', scatter_dimens...]
    dot_general x3 -> x0, matrix products: 30 us -> none  [the longest x1 24.1 us: body(): jnp.einsum('xt,xrd->trd', in_labels, incoming, preferred_element_type=jnp...]
    convert_element_type x3 -> x1, other arithmetic: 19.1 us -> 0.68 us  [body(): tab = jnp.concatenate([target_sector.T.astype(F32), coefficients.T], axis=0)]
    all_to_all x2 -> x0, starting transfers between devices: 15.9 us -> none  [the longest x1 8.45 us: body(): lax.all_to_all(labels, 'blk', split_axis=0, concat_axis=0, tiled=True)]
    select_n x3 -> x0, other arithmetic: 14 us -> none  [the longest x1 14 us: body(): jnp.where(filled[:, None, None], contribution[picked], jnp.zeros((), jnp....]
    gather x1 -> x0, local copies, waits for them, and re-layouts: 10.6 us -> none  [body(): contribution[picked]]
  transfers between devices with their start and end apart: 3 -> 0, of which waited for: 2 -> 0; matrix products, arithmetic and copies ran while one was open for 10% -> 0% of each run, Pallas kernels for 0% -> 0%
where the time goes in v1:
time: 146 us
  Pallas kernels  138 us (95%)
  local copies, waits for them, and re-layouts  6.01 us (4%)
    pallas_call x1, Pallas kernels, body(): pl.pallas_call(kernel, out_shape=(jax.ShapeDtypeStruct((4, 256, 1024), BF...  138 us
    unnamed x4, local copies, waits for them, and re-layouts  5.25 us

profile of v1, /device:TPU:0, one launch (start us, length us, event | category | flops | bytes accessed | tf_op | source)
XLA Modules:
  0.0 145.6 jit_solution(584182084364669260)
XLA Ops:
  0.6 0.7 convert_bitcast_fusion
  1.3 0.7 pad_maximum_fusion
  2.0 0.1 broadcast_in_dim.3
  2.1 0.1 reshape.7
  2.2 0.6 pad.4.tbl
  2.8 137.6 %recouple.1 = (bf16[4,256,1024]{2,1,0:T(8,128)(2,1)}, f32[4,1024,256]{2,1,0:T(8,128)}) custom-call(bf16[8,256,1024]{2,1,0:T(8,128)(2,1)} %src.1, f32[8,128]{1,0:T(8,128)} %pad.4.tbl), custom_call_target="tpu_custom_call" | custom-call | tf_op jit(solution)/shard_map/recouple/pallas_call | solution.py:281
  140.3 0.0 copy-start
  140.3 3.2 %copy.7 = bf16[4,256,1024]{2,1,0:T(8,128)(2,1)} copy(bf16[4,256,1024]{2,1,0:T(8,128)(2,1)} %get-tuple-element.4) | data formatting | bytes 4194304
  143.6 0.0 copy-done
  143.6 2.0 %copy.8 = f32[4,1024,256]{2,1,0:T(8,128)} copy(f32[4,1024,256]{2,1,0:T(8,128)S(1)} %copy-done) | data formatting | bytes 8388608
Async XLA Ops:
  140.3 3.2 %copy-start = (f32[4,1024,256]{2,1,0:T(8,128)S(1)}, f32[4,1024,256]{2,1,0:T(8,128)}, u32[]{:S(2)}) copy-start(f32[4,1024,256]{2,1,0:T(8,128)} %get-tuple-element.5) | copy-start | bytes 12582916

commit v2 on v1

--- a/solution.py
+++ b/solution.py
@@ -12,19 +12,20 @@
 F32 = jnp.float32
 
 ROWS = 16
-CW = 256
+CW = 128
 HALF = 128
 HCOL = 512
 NCC = HCOL // CW
 NCH = (HALF // ROWS) * NCC
-L_A2, L_CB, L_R2, L_FN, L_X2 = 2, 4, 6, 8, 10
+LOOK = 2
+L_CB, L_R2, L_FN, L_X2 = 2, 4, 6, 8
 STEPS = NCH + L_X2
 OFFS = (0, 1, 3, 2)
 
 
-def kernel(src, tbl, rec_out, den_out, G, TB, W, PS, T, F, Q, RG, D,
+def kernel(src, coef, targ, RG, G, MT, TB, W, PS, T, F, Q,
            s_in, s_a1, s_a2, s_r1, s_r2, s_d, s_x1, s_x2, s_t,
-           n_in, n_a1, n_a2, n_r1, n_r2, n_d, n_x1, n_x2, n_t, s_out):
+           n_in, n_a1, n_a2, n_r1, n_r2, n_d, n_x1, n_x2, n_t):
     blk = lax.axis_index("blk")
     x = lax.axis_index("rep")
     z = blk // 8
@@ -60,6 +61,15 @@
 
     def sent(ref, sem):
         waiter(ref, sem, s_d.at[0]).wait_send()
+
+    trow = lax.broadcasted_iota(jnp.int32, (8, 128), 0)
+    tblk = lax.broadcasted_iota(jnp.int32, (8, 128), 1) // ROWS
+    mt = jnp.zeros((8, 128), F32)
+    for k in range(2):
+        for b in range(8):
+            mt = jnp.where((trow == k) & (tblk == b), targ[k, b].astype(F32), mt)
+            mt = jnp.where((trow == k + 2) & (tblk == b), coef[k, b], mt)
+    MT[...] = mt
 
     peers = [partner]
     for k in (1, 2, 3):
@@ -81,14 +91,7 @@
         c0 = pl.multiple_of(cc * CW, CW)
         return r0, c0, pl.ds(r0, ROWS), pl.ds(c0, CW)
 
-    for p in range(2):
-        rcopy(tbl, TB.at[p, 0, c], n_t.at[0], s_t.at[0], partner)
-        for slot in (1, 2, 3):
-            for core in (0, 1):
-                rcopy(tbl, TB.at[p, slot, c], n_t.at[1], s_t.at[1],
-                      gather_at[p](OFFS[slot], core))
-
-    def load(q, carry):
+    def load(q):
         r0, c0, rows, cols = place(q)
         for p in range(2):
             cs = pl.ds(pl.multiple_of(p * HCOL + c0, CW), CW)
@@ -97,17 +100,16 @@
             dst = G.at[p, 0, pl.ds(c * 8, 8), rows, cols]
             pltpu.make_async_copy(mine, dst, s_in.at[q]).start()
             rcopy(other, dst, n_in.at[0], s_in.at[q], partner)
-        return carry
-
-    lax.fori_loop(0, NCH, load, 0)
 
     def stage_a1(q):
-        _, _, rows, cols = place(q)
-        got(G.at[:, 0, :, rows, cols], s_in.at[q])
-        for p in range(2):
-            mine = G.at[p, 0, :, rows, cols]
-            rcopy(mine, G.at[p, 1, :, rows, cols], n_a1.at[0], s_a1.at[q], gather_at[p](1, c))
-            rcopy(mine, G.at[p, 2, :, rows, cols], n_a1.at[1], s_a1.at[q], gather_at[p](3, c))
+        r0, c0, rows, cols = place(q)
+        own = pl.ds(c * 8, 8)
+        for p in range(2):
+            cs = pl.ds(pl.multiple_of(p * HCOL + c0, CW), CW)
+            for h in range(2):
+                part = src.at[:, pl.ds(pl.multiple_of(h * HALF + r0, ROWS), ROWS), cs]
+                rcopy(part, G.at[p, 1, own, rows, cols], n_a1.at[0], s_a1.at[q], gather_at[p](1, h))
+                rcopy(part, G.at[p, 2, own, rows, cols], n_a1.at[1], s_a1.at[q], gather_at[p](3, h))
 
     def stage_a2(q):
         _, _, rows, cols = place(q)
@@ -120,6 +122,7 @@
 
     def stage_cb(q):
         _, _, rows, cols = place(q)
+        got(G.at[:, 0, :, rows, cols], s_in.at[q])
         got(G.at[:, 3, :, rows, cols], s_a2.at[q])
         for p in range(2):
             s = G[p, :, :, rows, cols].reshape(64 * ROWS, CW)
@@ -179,13 +182,21 @@
         def _():
             stage(q)
 
-    stage_a1(0)
-    stage_a1(1)
+    for q in range(LOOK):
+        stage_a1(q)
+    for p in range(2):
+        rcopy(MT, TB.at[p, 0, c], n_t.at[0], s_t.at[0], partner)
+        for slot in (1, 2, 3):
+            for core in (0, 1):
+                rcopy(MT, TB.at[p, slot, c], n_t.at[1], s_t.at[1],
+                      gather_at[p](OFFS[slot], core))
+    for q in range(LOOK):
+        load(q)
 
     got(TB.at[:, 0, 0], s_t.at[0])
     got(TB.at[:, 1:4], s_t.at[1])
     for p in range(2):
-        TB[p, 0, c] = tbl[...]
+        TB[p, 0, c] = mt
     row = lax.broadcasted_iota(jnp.int32, (128, 128), 0)
     lane = lax.broadcasted_iota(jnp.int32, (128, 128), 1)
     same = (row % ROWS) == (lane % ROWS)
@@ -208,57 +219,24 @@
             lax.fori_loop(0, 8, build, 0)
 
     def step(s, carry):
-        run(stage_a1, s + 2)
-        run(stage_a2, s + 2 - L_A2)
-        run(stage_x2, s + 2 - L_X2)
-        run(stage_fn, s + 2 - L_FN)
-        run(stage_r2, s + 2 - L_R2)
-        run(stage_cb, s + 2 - L_CB)
+        run(stage_x2, s - L_X2)
+        run(stage_fn, s - L_FN)
+        run(stage_r2, s - L_R2)
+        run(stage_cb, s - L_CB)
+        run(stage_a2, s)
+        run(stage_a1, s + LOOK)
+        run(load, s + LOOK)
         return carry
 
-    lax.fori_loop(0, STEPS - 2, step, 0)
-
-    def last_d(q, carry):
+    lax.fori_loop(0, STEPS, step, 0)
+
+    def last(q, carry):
         _, _, rows, cols = place(q)
         got(RG.at[0, :, oc, :, rows, cols], s_d.at[q])
-        return carry
-
-    lax.fori_loop(0, NCH, last_d, 0)
-    outs = []
-    for h in range(2):
-        for p in range(2):
-            cp = pltpu.make_async_copy(
-                RG.at[0, :, h, p],
-                rec_out.at[:, h * HALF:(h + 1) * HALF, p * HCOL:(p + 1) * HCOL],
-                s_out.at[h * 2 + p])
-            cp.start()
-            outs.append(cp)
-
-    def last_x(q, carry):
-        _, _, rows, cols = place(q)
         got(RG.at[3, :, :, :, rows, cols], s_x2.at[q])
         return carry
 
-    lax.fori_loop(0, NCH, last_x, 0)
-
-    xp = x // 2
-    xo = pl.multiple_of((x % 2) * 256, 256)
-
-    def gram(w, carry):
-        rhs = RG[:, w, :, xp, :, pl.ds(xo, 256)].reshape(1024, 256)
-        for p in range(2):
-            lhs = RG[:, w, :, p].reshape(1024, HCOL)
-            D[w, p * HCOL:(p + 1) * HCOL, :] = lax.dot_general(
-                lhs, rhs, (((0,), (0,)), ((), ())), preferred_element_type=F32)
-        pltpu.make_async_copy(D.at[w], den_out.at[w], s_out.at[4 + w]).start()
-        return carry
-
-    lax.fori_loop(0, 4, gram, 0)
-
-    for w in range(4):
-        pltpu.make_async_copy(D.at[w], den_out.at[w], s_out.at[4 + w]).wait()
-    for cp in outs:
-        cp.wait()
+    lax.fori_loop(0, NCH, last, 0)
 
     sent(TB.at[:, 0, 0], n_t.at[0])
     sent(TB.at[:, 1:4], n_t.at[1])
@@ -273,39 +251,75 @@
     sent(Q, n_d.at[0])
 
 
+def finish(RG, rec_out, den_out, D, s_out):
+    x = lax.axis_index("rep")
+    outs = []
+    for h in range(2):
+        for p in range(2):
+            cp = pltpu.make_async_copy(
+                RG.at[0, :, h, p],
+                rec_out.at[:, h * HALF:(h + 1) * HALF, p * HCOL:(p + 1) * HCOL],
+                s_out.at[h * 2 + p])
+            cp.start()
+            outs.append(cp)
+    xp = x // 2
+    xo = pl.multiple_of((x % 2) * 256, 256)
+
+    def gram(w, carry):
+        rhs = RG[:, w, :, xp, :, pl.ds(xo, 256)].reshape(1024, 256)
+        for p in range(2):
+            lhs = RG[:, w, :, p].reshape(1024, HCOL)
+            D[w, p * HCOL:(p + 1) * HCOL, :] = lax.dot_general(
+                lhs, rhs, (((0,), (0,)), ((), ())), preferred_element_type=F32)
+        pltpu.make_async_copy(D.at[w], den_out.at[w], s_out.at[4 + w]).start()
+        return carry
+
+    lax.fori_loop(0, 4, gram, 0)
+    for w in range(4):
+        pltpu.make_async_copy(D.at[w], den_out.at[w], s_out.at[4 + w]).wait()
+    for cp in outs:
+        cp.wait()
+
+
 def body(source_blocks, coefficients, target_sector):
-    tab = jnp.concatenate([target_sector.T.astype(F32), coefficients.T], axis=0)
-    tab = jnp.pad(jnp.repeat(tab, ROWS, axis=1), ((0, 4), (0, 0)))
     dma = pltpu.SemaphoreType.DMA
     chunk_sems = [dma((NCH,)) for _ in range(8)]
-    return pl.pallas_call(
+    gathered = pl.pallas_call(
         kernel,
-        out_shape=(jax.ShapeDtypeStruct((4, 256, 1024), BF),
-                   jax.ShapeDtypeStruct((4, 1024, 256), F32)),
+        out_shape=pltpu.VMEM((4, 4, 2, 2, HALF, HCOL), BF),
         in_specs=[pl.BlockSpec(memory_space=pl.ANY),
-                  pl.BlockSpec(memory_space=pltpu.VMEM)],
-        out_specs=(pl.BlockSpec(memory_space=pl.ANY),
-                   pl.BlockSpec(memory_space=pl.ANY)),
+                  pl.BlockSpec(memory_space=pltpu.SMEM),
+                  pl.BlockSpec(memory_space=pltpu.SMEM)],
+        out_specs=pl.BlockSpec(memory_space=pltpu.VMEM),
         scratch_shapes=[
             pltpu.VMEM((2, 4, 16, HALF, HCOL), BF),
+            pltpu.VMEM((8, 128), F32),
             pltpu.VMEM((2, 4, 2, 8, 128), F32),
             pltpu.VMEM((2, 512, 1024), BF),
             pltpu.VMEM((2, 4, 8, HALF, HCOL), BF),
             pltpu.VMEM((2, 2, 4, HALF, HCOL), BF),
             pltpu.VMEM((2, 2, 8, HALF, HCOL), BF),
             pltpu.VMEM((4, 2, HALF, HCOL), BF),
-            pltpu.VMEM((4, 4, 2, 2, HALF, HCOL), BF),
-            pltpu.VMEM((4, 1024, 256), F32),
             *chunk_sems,
             dma((2,)),
             dma((1,)), dma((2,)), dma((2,)), dma((2,)), dma((2,)), dma((1,)),
             dma((2,)), dma((2,)), dma((2,)),
-            dma((8,)),
         ],
         compiler_params=pltpu.CompilerParams(
-            collective_id=0, has_side_effects=True, vmem_limit_bytes=64 * 1024 * 1024 - 65536),
+            collective_id=0, has_side_effects=True, vmem_limit_bytes=50 * 1024 * 1024),
         name="recouple",
-    )(source_blocks, tab)
+    )(source_blocks, coefficients.T, target_sector.T)
+    return pl.pallas_call(
+        finish,
+        out_shape=(jax.ShapeDtypeStruct((4, 256, 1024), BF),
+                   jax.ShapeDtypeStruct((4, 1024, 256), F32)),
+        in_specs=[pl.BlockSpec(memory_space=pltpu.VMEM)],
+        out_specs=(pl.BlockSpec(memory_space=pl.ANY),
+                   pl.BlockSpec(memory_space=pl.ANY)),
+        scratch_shapes=[pltpu.VMEM((4, 1024, 256), F32), dma((8,))],
+        compiler_params=pltpu.CompilerParams(vmem_limit_bytes=24 * 1024 * 1024),
+        name="finish",
+    )(gathered)
 
 
 def solution(mesh):

time: 146 us -> 138 us (0.945)
  local copies, waits for them, and re-layouts: 6.01 us -> 0 us
    unnamed x4 -> x0, local copies, waits for them, and re-layouts: 5.25 us -> none
    pallas_call x1 -> x2, Pallas kernels: 138 us -> 137 us  [the longest x1 133 us: body(): pl.pallas_call(kernel, out_shape=pltpu.VMEM((4, 4, 2, 2, HALF, HCOL), BF)...]
where the time goes in v2:
time: 138 us
  Pallas kernels  137 us (99%)
    pallas_call x1, Pallas kernels, body(): pl.pallas_call(kernel, out_shape=pltpu.VMEM((4, 4, 2, 2, HALF, HCOL), BF)...  133 us
    pallas_call x1, Pallas kernels, body(): pl.pallas_call(finish, out_shape=(jax.ShapeDtypeStruct((4, 256, 1024), BF...  4.09 us

profile of v2, /device:TPU:0, one launch (start us, length us, event | category | flops | bytes accessed | tf_op | source)
XLA Modules:
  0.0 137.7 jit_solution(12401081365628028359)
XLA Ops:
  0.6 132.9 %recouple.1.RG = bf16[4,4,2,2,128,512]{5,4,3,2,1,0:T(8,128)(2,1)S(1)} custom-call(bf16[8,256,1024]{2,1,0:T(8,128)(2,1)} %src.1, f32[2,8]{1,0:T(2,128)} %bitcast.2, s32[2,8]{1,0:T(2,128)} %bitcast.3), custom_call_target="tpu_custom_call" | custom-call | tf_op jit(solution)/shard_map/recouple/pallas_call | solution.py:287
  133.6 4.1 %finish.1 = (bf16[4,256,1024]{2,1,0:T(8,128)(2,1)}, f32[4,1024,256]{2,1,0:T(8,128)}) custom-call(bf16[4,4,2,2,128,512]{5,4,3,2,1,0:T(8,128)(2,1)S(1)} %recouple.1.RG), custom_call_target="tpu_custom_call" | custom-call | tf_op jit(solution)/shard_map/finish/pallas_call | solution.py:312

commit v3 on v2

--- a/solution.py
+++ b/solution.py
@@ -17,15 +17,18 @@
 HCOL = 512
 NCC = HCOL // CW
 NCH = (HALF // ROWS) * NCC
-LOOK = 2
-L_CB, L_R2, L_FN, L_X2 = 2, 4, 6, 8
-STEPS = NCH + L_X2
+A1, A2, PRE = 6, 2, 6
+L_R2, L_FN, L_X2, L_X3 = 2, 4, 6, 8
+STEPS = NCH + L_X3
+KROWS = 32
+GCH = (KROWS // ROWS) * NCC
+KCON = 8 * KROWS
 OFFS = (0, 1, 3, 2)
 
 
-def kernel(src, coef, targ, RG, G, MT, TB, W, PS, T, F, Q,
+def kernel(src, coef_h, targ_h, RG, D, coef, targ, G, MT, TB, W, PS, T, F, Q,
            s_in, s_a1, s_a2, s_r1, s_r2, s_d, s_x1, s_x2, s_t,
-           n_in, n_a1, n_a2, n_r1, n_r2, n_d, n_x1, n_x2, n_t):
+           n_in, n_a1, n_a2, n_r1, n_r2, n_d, n_x1, n_x2, n_t, s_sm):
     blk = lax.axis_index("blk")
     x = lax.axis_index("rep")
     z = blk // 8
@@ -61,15 +64,6 @@
 
     def sent(ref, sem):
         waiter(ref, sem, s_d.at[0]).wait_send()
-
-    trow = lax.broadcasted_iota(jnp.int32, (8, 128), 0)
-    tblk = lax.broadcasted_iota(jnp.int32, (8, 128), 1) // ROWS
-    mt = jnp.zeros((8, 128), F32)
-    for k in range(2):
-        for b in range(8):
-            mt = jnp.where((trow == k) & (tblk == b), targ[k, b].astype(F32), mt)
-            mt = jnp.where((trow == k + 2) & (tblk == b), coef[k, b], mt)
-    MT[...] = mt
 
     peers = [partner]
     for k in (1, 2, 3):
@@ -82,6 +76,22 @@
     barrier = pltpu.get_barrier_semaphore()
     for dev in peers:
         pl.semaphore_signal(barrier, inc=1, device_id=dev, device_id_type=MESH)
+    small = [pltpu.make_async_copy(coef_h, coef, s_sm.at[0]),
+             pltpu.make_async_copy(targ_h, targ, s_sm.at[1])]
+    for cp in small:
+        cp.start()
+    for cp in small:
+        cp.wait()
+
+    trow = lax.broadcasted_iota(jnp.int32, (8, 128), 0)
+    tblk = lax.broadcasted_iota(jnp.int32, (8, 128), 1) // ROWS
+    mt = jnp.zeros((8, 128), F32)
+    for k in range(2):
+        for b in range(8):
+            mt = jnp.where((trow == k) & (tblk == b), targ[k, b].astype(F32), mt)
+            mt = jnp.where((trow == k + 2) & (tblk == b), coef[k, b], mt)
+    MT[...] = mt
+
     pl.semaphore_wait(barrier, len(peers))
 
     def place(q):
@@ -177,66 +187,90 @@
         rcopy(RG.at[2, :, 1, :, rows, cols], RG.at[3, :, 1, :, rows, cols],
               n_x2.at[1], s_x2.at[q], at_x(3, c))
 
-    def run(stage, q):
-        @pl.when((q >= 0) & (q < NCH))
+    def stage_x3(q):
+        _, _, rows, cols = place(q)
+        got(RG.at[0, :, oc, :, rows, cols], s_d.at[q])
+        got(RG.at[3, :, :, :, rows, cols], s_x2.at[q])
+
+    xp = x // 2
+    xo = pl.multiple_of((x % 2) * 256, 256)
+
+    def gram(g, w):
+        rows = pl.ds(pl.multiple_of(g * KROWS, KROWS), KROWS)
+        rhs = RG[:, w, :, xp, rows, pl.ds(xo, 256)].reshape(KCON, 256)
+        for p in range(2):
+            lhs = RG[:, w, :, p, rows, :].reshape(KCON, HCOL)
+            part = lax.dot_general(
+                lhs, rhs, (((0,), (0,)), ((), ())), preferred_element_type=F32)
+            at = slice(p * HCOL, (p + 1) * HCOL)
+
+            @pl.when(g == 0)
+            def _():
+                D[w, at, :] = part
+
+            @pl.when(g > 0)
+            def _():
+                D[w, at, :] += part
+
+    def run(stage, q, least=0):
+        @pl.when((q >= least) & (q < NCH))
         def _():
             stage(q)
 
-    for q in range(LOOK):
-        stage_a1(q)
     for p in range(2):
         rcopy(MT, TB.at[p, 0, c], n_t.at[0], s_t.at[0], partner)
         for slot in (1, 2, 3):
             for core in (0, 1):
                 rcopy(MT, TB.at[p, slot, c], n_t.at[1], s_t.at[1],
                       gather_at[p](OFFS[slot], core))
-    for q in range(LOOK):
+    for q in range(PRE):
+        stage_a1(q)
+    for q in range(PRE):
         load(q)
+    for q in range(A2):
+        stage_a2(q)
 
     got(TB.at[:, 0, 0], s_t.at[0])
     got(TB.at[:, 1:4], s_t.at[1])
     for p in range(2):
         TB[p, 0, c] = mt
-    row = lax.broadcasted_iota(jnp.int32, (128, 128), 0)
-    lane = lax.broadcasted_iota(jnp.int32, (128, 128), 1)
-    same = (row % ROWS) == (lane % ROWS)
-    sect = row // ROWS
+    row = lax.broadcasted_iota(jnp.int32, (128, 128), 0).astype(F32)
+    lane = (lax.broadcasted_iota(jnp.int32, (1, 128), 1) % ROWS).astype(F32)
     for p in range(2):
         for d in range(4):
             if p == 0:
                 base = (z * 4 + (y + OFFS[d]) % 4) * 8
             else:
                 base = (((z + OFFS[d]) % 4) * 4 + y) * 8
-            want = (sect + base).astype(F32)
-
-            def build(jk, carry, p=p, d=d, want=want):
+            base = base.astype(F32)
+
+            def build(jk, carry, p=p, d=d, base=base):
                 tab = TB[p, jk // 2, jk % 2]
-                w = jnp.where(same & (tab[0:1, :] == want), tab[2:3, :], 0.0)
-                w = w + jnp.where(same & (tab[1:2, :] == want), tab[3:4, :], 0.0)
+                i0 = (tab[0:1, :] - base) * ROWS + lane
+                i1 = (tab[1:2, :] - base) * ROWS + lane
+                w = jnp.where(row == i0, tab[2:3, :], jnp.where(row == i1, tab[3:4, :], 0.0))
                 W[p, d * 128:(d + 1) * 128, pl.ds(pl.multiple_of(jk * 128, 128), 128)] = w.astype(BF)
                 return carry
 
             lax.fori_loop(0, 8, build, 0)
 
     def step(s, carry):
+        run(stage_a1, s + A1, PRE)
+        run(stage_a2, s + A2)
+        run(stage_cb, s)
+        run(stage_r2, s - L_R2)
+        run(stage_fn, s - L_FN)
         run(stage_x2, s - L_X2)
-        run(stage_fn, s - L_FN)
-        run(stage_r2, s - L_R2)
-        run(stage_cb, s - L_CB)
-        run(stage_a2, s)
-        run(stage_a1, s + LOOK)
-        run(load, s + LOOK)
+        run(stage_x3, s - L_X3)
+        run(load, s + A1, PRE)
+        piece = s - (GCH + L_X3)
+
+        @pl.when((piece >= 0) & (piece % GCH < 4) & (piece // GCH < HALF // KROWS - 1))
+        def _():
+            gram(piece // GCH, piece % GCH)
         return carry
 
     lax.fori_loop(0, STEPS, step, 0)
-
-    def last(q, carry):
-        _, _, rows, cols = place(q)
-        got(RG.at[0, :, oc, :, rows, cols], s_d.at[q])
-        got(RG.at[3, :, :, :, rows, cols], s_x2.at[q])
-        return carry
-
-    lax.fori_loop(0, NCH, last, 0)
 
     sent(TB.at[:, 0, 0], n_t.at[0])
     sent(TB.at[:, 1:4], n_t.at[1])
@@ -251,7 +285,7 @@
     sent(Q, n_d.at[0])
 
 
-def finish(RG, rec_out, den_out, D, s_out):
+def finish(RG, D_in, rec_out, den_out, D, s_out):
     x = lax.axis_index("rep")
     outs = []
     for h in range(2):
@@ -264,12 +298,14 @@
             outs.append(cp)
     xp = x // 2
     xo = pl.multiple_of((x % 2) * 256, 256)
+    rows = slice(HALF - KROWS, HALF)
 
     def gram(w, carry):
-        rhs = RG[:, w, :, xp, :, pl.ds(xo, 256)].reshape(1024, 256)
-        for p in range(2):
-            lhs = RG[:, w, :, p].reshape(1024, HCOL)
-            D[w, p * HCOL:(p + 1) * HCOL, :] = lax.dot_general(
+        rhs = RG[:, w, :, xp, rows, pl.ds(xo, 256)].reshape(KCON, 256)
+        for p in range(2):
+            lhs = RG[:, w, :, p, rows, :].reshape(KCON, HCOL)
+            at = slice(p * HCOL, (p + 1) * HCOL)
+            D[w, at, :] = D_in[w, at, :] + lax.dot_general(
                 lhs, rhs, (((0,), (0,)), ((), ())), preferred_element_type=F32)
         pltpu.make_async_copy(D.at[w], den_out.at[w], s_out.at[4 + w]).start()
         return carry
@@ -284,14 +320,18 @@
 def body(source_blocks, coefficients, target_sector):
     dma = pltpu.SemaphoreType.DMA
     chunk_sems = [dma((NCH,)) for _ in range(8)]
-    gathered = pl.pallas_call(
+    gathered, partial = pl.pallas_call(
         kernel,
-        out_shape=pltpu.VMEM((4, 4, 2, 2, HALF, HCOL), BF),
+        out_shape=(pltpu.VMEM((4, 4, 2, 2, HALF, HCOL), BF),
+                   pltpu.VMEM((4, 1024, 256), F32)),
         in_specs=[pl.BlockSpec(memory_space=pl.ANY),
-                  pl.BlockSpec(memory_space=pltpu.SMEM),
-                  pl.BlockSpec(memory_space=pltpu.SMEM)],
-        out_specs=pl.BlockSpec(memory_space=pltpu.VMEM),
+                  pl.BlockSpec(memory_space=pl.ANY),
+                  pl.BlockSpec(memory_space=pl.ANY)],
+        out_specs=(pl.BlockSpec(memory_space=pltpu.VMEM),
+                   pl.BlockSpec(memory_space=pltpu.VMEM)),
         scratch_shapes=[
+            pltpu.SMEM((2, 8), F32),
+            pltpu.SMEM((2, 8), jnp.int32),
             pltpu.VMEM((2, 4, 16, HALF, HCOL), BF),
             pltpu.VMEM((8, 128), F32),
             pltpu.VMEM((2, 4, 2, 8, 128), F32),
@@ -304,22 +344,24 @@
             dma((2,)),
             dma((1,)), dma((2,)), dma((2,)), dma((2,)), dma((2,)), dma((1,)),
             dma((2,)), dma((2,)), dma((2,)),
+            dma((2,)),
         ],
         compiler_params=pltpu.CompilerParams(
-            collective_id=0, has_side_effects=True, vmem_limit_bytes=50 * 1024 * 1024),
+            collective_id=0, has_side_effects=True, vmem_limit_bytes=46 * 1024 * 1024),
         name="recouple",
     )(source_blocks, coefficients.T, target_sector.T)
     return pl.pallas_call(
         finish,
         out_shape=(jax.ShapeDtypeStruct((4, 256, 1024), BF),
                    jax.ShapeDtypeStruct((4, 1024, 256), F32)),
-        in_specs=[pl.BlockSpec(memory_space=pltpu.VMEM)],
+        in_specs=[pl.BlockSpec(memory_space=pltpu.VMEM),
+                  pl.BlockSpec(memory_space=pltpu.VMEM)],
         out_specs=(pl.BlockSpec(memory_space=pl.ANY),
                    pl.BlockSpec(memory_space=pl.ANY)),
         scratch_shapes=[pltpu.VMEM((4, 1024, 256), F32), dma((8,))],
         compiler_params=pltpu.CompilerParams(vmem_limit_bytes=24 * 1024 * 1024),
         name="finish",
-    )(gathered)
+    )(gathered, partial)
 
 
 def solution(mesh):

time: 138 us -> 132 us (0.957)
  Pallas kernels: 137 us -> 131 us
    pallas_call x1, Pallas kernels: 133 us -> 128 us  [body(): pl.pallas_call(kernel, out_shape=(pltpu.VMEM((4, 4, 2, 2, HALF, HCOL), BF...]
where the time goes in v3:
time: 132 us
  Pallas kernels  131 us (99%)
    pallas_call x1, Pallas kernels, body(): pl.pallas_call(kernel, out_shape=(pltpu.VMEM((4, 4, 2, 2, HALF, HCOL), BF...  128 us
    pallas_call x1, Pallas kernels, body(): pl.pallas_call(finish, out_shape=(jax.ShapeDtypeStruct((4, 256, 1024), BF...  2.75 us

profile of v3, /device:TPU:0, one launch (start us, length us, event | category | flops | bytes accessed | tf_op | source)
XLA Modules:
  0.0 131.6 jit_solution(13946731856227065355)
XLA Ops:
  0.6 128.2 %recouple.1 = (bf16[4,4,2,2,128,512]{5,4,3,2,1,0:T(8,128)(2,1)S(1)}, f32[4,1024,256]{2,1,0:T(8,128)S(1)}) custom-call(bf16[8,256,1024]{2,1,0:T(8,128)(2,1)} %src.1, f32[2,8]{1,0:T(2,128)} %bitcast.2, s32[2,8]{1,0:T(2,128)} %bitcast.3), custom_call_target="tpu_custom_call" | custom-call | tf_op jit(solution)/shard_map/recouple/pallas_call | solution.py:323
  128.8 2.7 %finish.1 = (bf16[4,256,1024]{2,1,0:T(8,128)(2,1)}, f32[4,1024,256]{2,1,0:T(8,128)}) custom-call(bf16[4,4,2,2,128,512]{5,4,3,2,1,0:T(8,128)(2,1)S(1)} %get-tuple-element.4.RG, f32[4,1024,256]{2,1,0:T(8,128)S(1)} %get-tuple-element.5.D_in), custom_call_target="tpu_custom_call" | custom-call | tf_op jit(solution)/shard_map/finish/pallas_call | solution.py:353
